TPU v7x, 32 devices: a whole 2x2x4 slice. The times are simulated.
32 devices in a mesh: robot: 8 (over z, x), sub: 4 (over y, core).
Axes of the slice: x: 2, y: 2, z: 4, core: 2. Of those that a mesh axis runs over, the one named last changes fastest.
Arguments:
- landmark_copies: float32 [8, 4, 3, 512], P('robot', 'sub'), may hold values from -6 to 6
- dual_copies: float32 [8, 4, 3, 512], P('robot', 'sub'), may hold values from -4 to 4
- visibility: int32 [8, 4, 512], P('robot', 'sub'), may hold values from 0 to 511
- block_counts: int32 [8, 4, 8], P('robot', 'sub'), may hold values from 1 to 64, as said below
- consensus_old: float32 [8, 4, 3, 512], P('robot', 'sub'), may hold values from -6 to 6
- poses: float32 [8, 4, 6, 1024], P('robot', 'sub'), may hold values from -6 to 6
- inverse_blocks: float32 [8, 4, 36, 1024], P('robot', 'sub'), may hold values from -1.8 to 1.8
- jacobians: float32 [8, 4, 18, 4096], P('robot', 'sub'), may hold values from -3 to 3
- measurements: float32 [8, 4, 3, 4096], P('robot', 'sub'), may hold values from -6 to 6
- obs_pose: int32 [8, 4, 4096], P('robot', 'sub'), may hold values from 0 to 1023
- obs_slot: int32 [8, 4, 4096], P('robot', 'sub'), may hold values from 0 to 511, as said below
- edge_to: int32 [8, 4, 1024], P('robot', 'sub'), may hold values from 0 to 4095
- edge_offset: float32 [8, 4, 6, 1024], P('robot', 'sub'), may hold values from -3 to 3
Outputs:
- refined_poses: float32 [8, 4, 6, 1024], P('robot', 'sub')
- consensus: float32 [8, 4, 3, 512], P('robot', 'sub')
- dual_new: float32 [8, 4, 3, 512], P('robot', 'sub')
- residual_norms: float32 [2], replicated
Inputs may be any that keep to these rules, and one draw needn't show every extreme that they name: block_counts[r,s,d] counts the live slots at the head of block d; for every sub index some robot receives full blocks from every robot, which robot varies with the draw. `obs_slot`: each observation names a live slot of its own device.
All inputs are finite; a program needn't handle non-finite values.
Results may differ from a plain program's by a relative error of at most 0.0001.
Values sent between devices are 32-bit elements; how exact they have to be, the bound alone decides.
No kernel may reach another device: no remote copies, remote signals or barrier semaphores. Data moves between devices by JAX's collectives and lax.ppermute only.
A program may use at most 64 MiB of HBM per device.

v0:
```python
import jax
import jax.numpy as jnp
from jax import lax
from jax.sharding import PartitionSpec as P

penalty = 2.0


def body(
    landmark_copies,
    dual_copies,
    visibility,
    block_counts,
    consensus_old,
    poses,
    inverse_blocks,
    jacobians,
    measurements,
    obs_pose,
    obs_slot,
    edge_to,
    edge_offset,
):
    copies = landmark_copies[0, 0]
    duals = dual_copies[0, 0]
    slot_ids = visibility[0]
    counts = block_counts[0, 0]
    old_estimate = consensus_old[0, 0]
    robots = lax.axis_size("robot")
    slot_count = copies.shape[1]
    block_size = slot_count // robots
    owned = old_estimate.shape[1]
    live_mask = (
        (jnp.arange(block_size)[None, :] < counts[:, None]).reshape(slot_count).astype(jnp.float32)
    )
    outgoing = jnp.concatenate([(copies + duals) * live_mask[None, :], live_mask[None, :]], axis=0)
    received, received_ids = (
        lax.all_to_all(outgoing, "robot", split_axis=1, concat_axis=1, tiled=True),
        lax.all_to_all(slot_ids, "robot", split_axis=1, concat_axis=1, tiled=True),
    )
    owner_ids = received_ids[0]
    totals = jax.vmap(lambda entries: jax.ops.segment_sum(entries, owner_ids, num_segments=owned))(
        received
    )
    consensus = (old_estimate + totals[:3]) / (1.0 + totals[3:4])
    returning = consensus[:, owner_ids]
    back = lax.all_to_all(returning, "robot", split_axis=1, concat_axis=1, tiled=True)
    differ = (copies - back) * live_mask[None, :]
    dual_new = duals + differ
    primal = jnp.sum(differ * differ)
    change = consensus - old_estimate
    dualsum = penalty * penalty * jnp.sum(totals[3:4] * change * change)
    primal_all, dual_all = lax.psum((primal, dualsum), ("robot", "sub"))
    landmark_total = owned * robots * lax.axis_size("sub")
    residual_norms = jnp.sqrt(jnp.stack([primal_all, dual_all]) / landmark_total)
    pose_block = poses[0, 0]
    pose_count = pose_block.shape[1]
    robot_all = lax.all_gather(pose_block, "sub", axis=1, tiled=True)
    pose_far = robot_all[:, edge_to[0, 0]]
    copies_at = copies[:, obs_slot[0, 0]]
    error = measurements[0, 0] - copies_at
    jac_rows = jacobians[0, 0].reshape(3, 6, error.shape[1])
    pull = jnp.sum(jac_rows * error[:, None, :], axis=0)
    pose_ids = obs_pose[0, 0]
    grad_obs = jax.vmap(
        lambda entries: jax.ops.segment_sum(entries, pose_ids, num_segments=pose_count)
    )(pull)
    grad = grad_obs + pose_far - pose_block - edge_offset[0, 0]
    inverse = inverse_blocks[0, 0].reshape(6, 6, pose_count)
    delta = jnp.sum(inverse * grad[None, :, :], axis=1)
    refined = pose_block + delta
    return (refined[None, None], consensus[None, None], dual_new[None, None], residual_norms)


def solution(mesh):
    return jax.shard_map(
        body,
        mesh=mesh,
        in_specs=(
            P("robot", "sub", None, None),
            P("robot", "sub", None, None),
            P("robot", "sub", None),
            P("robot", "sub", None),
            P("robot", "sub", None, None),
            P("robot", "sub", None, None),
            P("robot", "sub", None, None),
            P("robot", "sub", None, None),
            P("robot", "sub", None, None),
            P("robot", "sub", None),
            P("robot", "sub", None),
            P("robot", "sub", None),
            P("robot", "sub", None, None),
        ),
        out_specs=(
            P("robot", "sub", None, None),
            P("robot", "sub", None, None),
            P("robot", "sub", None, None),
            P(),
        ),
        check_vma=False,
    )
```

profile of v0, /device:TPU:0, one launch (start us, length us, event | category | flops | bytes accessed | tf_op | source)
XLA Modules:
  0.0 154.9 jit_solution(5562532823633209940)
XLA Ops:
  1.1 1.3 reduce.16
  3.2 7.3 %all-to-all-start = ((s32[1,8,64]{2,0,1:T(1,128)}), s32[1,8,64]{2,0,1:T(1,128)S(1)}, u32[]{:S(2)}, u32[]{:S(2)}) async-start(s32[1,8,64]{2,0,1:T(1,128)} %all_to_all.22), calls=%async_computation | async-start | bytes 8192 | tf_op jit(solution)/shard_map/all_to_all | solution.py:39
  11.9 0.8 copy.53
  12.7 0.7 add_reduce_fusion.1
  13.6 0.7 compare_select_fusion
  14.3 1.4 copy.52
  15.7 14.1 %gather_fusion.1 = f32[4096,3]{1,0:T(8,128)} fusion(f32[3,512]{0,1:T(8,128)S(1)} %bitcast.54, s32[4096]{0:T(1024)S(1)} %broadcast_clamp_fusion), kind=kCustom, calls=%fused_computation.1 | custom fusion | bytes 114688 | tf_op jit(solution)/shard_map/gather | solution.py:60
  29.8 3.2 %bitcast_subtract_fusion = f32[3,4096]{0,1:T(8,128)} fusion(f32[4096,3]{1,0:T(8,128)} %gather_fusion.1, f32[1,1,3,4096]{2,3,1,0:T(8,128)S(1)} %copy.52), kind=kLoop, calls=%fused_computation.5 | loop fusion | flops 12288 | bytes 147456 | tf_op jit(solution)/shard_map/sub | solution.py:61
  33.0 2.3 %copy.54 = f32[3,4096]{1,0:T(4,128)S(1)} copy(f32[3,4096]{0,1:T(8,128)} %bitcast_subtract_fusion) | data formatting | bytes 98304 | tf_op jit(solution)/shard_map/sub | solution.py:61
  36.1 2.0 %copy.55 = f32[4096,6]{1,0:T(8,128)} copy(f32[4096,6]{0,1:T(8,128)S(1)} %bitcast.57) | data formatting | bytes 196608 | tf_op jit(solution)/shard_map/reduce_sum | solution.py:63
  38.3 15.8 %all-gather = f32[1,1,6,4096]{2,3,1,0:T(8,128)S(1)} all-gather(f32[1,1,6,1024]{2,3,1,0:T(8,128)S(1)} %copy.51), channel_id=2, replica_groups=mesh['robot'=8,'sub'=4] {'sub'}, dimensions={3}, use_global_device_ids=true | all-gather | bytes 122880 | tf_op jit(solution)/shard_map/all_gather | solution.py:58
  54.1 1.0 copy.57
  55.1 2.8 %gather_fusion = f32[1024,6]{1,0:T(8,128)S(1)} fusion(f32[6,4096]{0,1:T(8,128)S(1)} %bitcast.55, s32[1024]{0:T(1024)S(1)} %broadcast_clamp_fusion.1), kind=kCustom, calls=%fused_computation | custom fusion | bytes 53248 | tf_op jit(solution)/shard_map/gather | solution.py:59
  58.0 22.9 %scatter_fusion = f32[6,1024]{0,1:T(8,128)S(1)} fusion(f32[6,1024]{0,1:T(8,128)S(1)} %bitcast.53, s32[4096]{0:T(1024)S(1)} %bitcast.67, f32[4096,6]{1,0:T(8,128)} %copy.55), kind=kCustom, calls=%fused_computation.3 | custom fusion | flops 24576 | bytes 311296 | tf_op jit(solution)/shard_map/vmap()/scatter-add | solution.py:66
  82.6 6.0 %all-to-all-start.1 = ((f32[8,1,256]{2,1,0:T(1,128)}), f32[8,1,256]{2,1,0:T(1,128)S(1)}, u32[]{:S(2)}, u32[]{:S(2)}) async-start(f32[8,1,256]{2,1,0:T(1,128)} %reshape.262), calls=%async_computation.1 | async-start | bytes 16384 | tf_op jit(solution)/shard_map/all_to_all | solution.py:38
  89.4 5.7 %all-to-all-done.1 = f32[8,1,256]{2,1,0:T(1,128)S(1)} async-done(((f32[8,1,256]{2,1,0:T(1,128)}), f32[8,1,256]{2,1,0:T(1,128)S(1)}, u32[]{:S(2)}, u32[]{:S(2)}) %all-to-all-start.1) | async-done | bytes 8224 | tf_op jit(solution)/shard_map/all_to_all | solution.py:38
  96.6 2.3 %scatter_custom_fusion.1 = f32[4,512]{0,1:T(8,128)S(1)} fusion(s32[512]{0:T(512)S(1)} %reshape.227, f32[512,4]{1,0:T(8,128)S(1)} %copy.62, f32[]{:T(128)} %constant.10.clone.1), kind=kCustom, calls=%fused_computation.21 | custom fusion | flops 2048 | bytes 8196 | tf_op jit(solution)/shard_map/vmap()/scatter-add | solution.py:42
  99.2 0.8 fusion
  100.0 1.0 gather_fusion.2
  101.9 3.3 %all-to-all-start.2 = ((f32[8,1,192]{2,1,0:T(1,128)}), f32[8,1,192]{2,1,0:T(1,128)S(1)}, u32[]{:S(2)}, u32[]{:S(2)}) async-start(f32[8,1,192]{2,1,0:T(1,128)} %reshape.264), calls=%async_computation.2 | async-start | bytes 16384 | tf_op jit(solution)/shard_map/all_to_all | solution.py:47
  107.3 4.4 %all-to-all-done.2 = f32[8,1,192]{2,1,0:T(1,128)S(1)} async-done(((f32[8,1,192]{2,1,0:T(1,128)}), f32[8,1,192]{2,1,0:T(1,128)S(1)}, u32[]{:S(2)}, u32[]{:S(2)}) %all-to-all-start.2) | async-done | bytes 6176 | tf_op jit(solution)/shard_map/all_to_all | solution.py:47
  112.7 0.7 fusion.4
  114.1 38.9 %all-reduce = (f32[1]{0:T(128)}, f32[1]{0:T(128)}) all-reduce(f32[1]{0:T(128)} %bitcast.22, f32[1]{0:T(128)} %bitcast.21), channel_id=1, replica_groups=mesh['robot'=8,'sub'=4] {'robot','sub'}, use_global_device_ids=true, to_apply=%region_7.0 | all-reduce | flops 2 | bytes 16 | tf_op jit(solution)/shard_map/psum | solution.py:53
  153.0 1.9 %fusion.10 = f32[2]{0:T(128)} fusion(f32[1]{0:T(128)} %get-tuple-element.22, f32[1]{0:T(128)} %get-tuple-element.23), kind=kLoop, calls=%fused_computation.41 | loop fusion | flops 4 | bytes 16 | tf_op jit(solution)/shard_map/sqrt | solution.py:55
  (67 shorter events, 11.8 us)
Async XLA Ops:
  3.2 79.4 %all-to-all-start = ((s32[1,8,64]{2,0,1:T(1,128)}), s32[1,8,64]{2,0,1:T(1,128)S(1)}, u32[]{:S(2)}, u32[]{:S(2)}) async-start(s32[1,8,64]{2,0,1:T(1,128)} %all_to_all.22), calls=%async_computation | async-start | bytes 8192 | tf_op jit(solution)/shard_map/all_to_all | solution.py:39
  33.0 2.3 %copy-start.1 = (f32[1,1,18,4096]{3,1,2,0:T(1,128)S(1)}, f32[1,1,18,4096]{3,1,2,0:T(1,128)}, u32[]{:S(2)}) copy-start(f32[1,1,18,4096]{3,1,2,0:T(1,128)} %param.20) | copy-start | bytes 884740
  35.2 2.8 %copy-start.3 = (f32[1,1,6,1024]{3,1,2,0:T(1,128)S(1)}, f32[1,1,6,1024]{3,1,2,0:T(1,128)}, u32[]{:S(2)}) copy-start(f32[1,1,6,1024]{3,1,2,0:T(1,128)} %param.18) | copy-start | bytes 73732
  38.1 16.0 %copy-start.9 = (s32[1,1,1024]{2,1,0:T(1,128)S(1)}, s32[1,1,1024]{2,1,0:T(1,128)}, u32[]{:S(2)}) copy-start(s32[1,1,1024]{2,1,0:T(1,128)} %param.24) | copy-start | bytes 12292
  38.1 16.0 %copy-start.5 = (f32[1,1,6,1024]{3,1,2,0:T(1,128)S(1)}, f32[1,1,6,1024]{3,1,2,0:T(1,128)}, u32[]{:S(2)}) copy-start(f32[1,1,6,1024]{3,1,2,0:T(1,128)} %param.25) | copy-start | bytes 73732
  38.1 19.9 %copy-start.7 = (s32[1,1,4096]{2,1,0:T(1,128)S(1)}, s32[1,1,4096]{2,1,0:T(1,128)}, u32[]{:S(2)}) copy-start(s32[1,1,4096]{2,1,0:T(1,128)} %param.22) | copy-start | bytes 49156
  57.9 23.0 %copy-start = (f32[1,1,6,1024]{2,3,1,0:T(8,128)S(1)}, f32[1,1,6,1024]{2,3,1,0:T(8,128)}, u32[]{:S(2)}) copy-start(f32[1,1,6,1024]{2,3,1,0:T(8,128)} %copy.57) | copy-start | bytes 73732
  58.0 23.2 %copy-start.2 = (f32[1,1,36,1024]{3,1,2,0:T(1,128)S(1)}, f32[1,1,36,1024]{3,1,2,0:T(1,128)}, u32[]{:S(2)}) copy-start(f32[1,1,36,1024]{3,1,2,0:T(1,128)} %param.19) | copy-start | bytes 442372
  80.9 1.5 copy-start.8
  81.6 31.9 %copy-start.4 = (f32[1,1,3,512]{3,1,2,0:T(1,128)S(1)}, f32[1,1,3,512]{3,1,2,0:T(1,128)}, u32[]{:S(2)}) copy-start(f32[1,1,3,512]{3,1,2,0:T(1,128)} %param.13) | copy-start | bytes 18436
  81.6 31.9 %copy-start.6 = (f32[1,1,3,512]{3,1,2,0:T(1,128)S(1)}, f32[1,1,3,512]{3,1,2,0:T(1,128)}, u32[]{:S(2)}) copy-start(f32[1,1,3,512]{3,1,2,0:T(1,128)} %param.14) | copy-start | bytes 18436
  82.6 12.5 %all-to-all-start.1 = ((f32[8,1,256]{2,1,0:T(1,128)}), f32[8,1,256]{2,1,0:T(1,128)S(1)}, u32[]{:S(2)}, u32[]{:S(2)}) async-start(f32[8,1,256]{2,1,0:T(1,128)} %reshape.262), calls=%async_computation.1 | async-start | bytes 16384 | tf_op jit(solution)/shard_map/all_to_all | solution.py:38
  101.9 9.8 %all-to-all-start.2 = ((f32[8,1,192]{2,1,0:T(1,128)}), f32[8,1,192]{2,1,0:T(1,128)S(1)}, u32[]{:S(2)}, u32[]{:S(2)}) async-start(f32[8,1,192]{2,1,0:T(1,128)} %reshape.264), calls=%async_computation.2 | async-start | bytes 16384 | tf_op jit(solution)/shard_map/all_to_all | solution.py:47
where the time goes:
time: 156 us; the launch traced here: 155 us
  blocking collectives  54.7 us (35%)
  other arithmetic  40.4 us (26%)
  local copies, waits for them, and re-layouts  31.6 us (20%)
  starting transfers between devices  16.6 us (11%)
  waiting for transfers between devices  10.1 us (6%)
  between operations  1.6 us (1%)
    psum x1, blocking collectives, body(): primal_all, dual_all = lax.psum((primal, dualsum), ('robot', 'sub'))  38.9 us
    scatter-add x1, other arithmetic, body(): jax.ops.segment_sum(entries, pose_ids, num_segments=pose_count)  22.9 us
    all_gather x1, blocking collectives, body(): robot_all = lax.all_gather(pose_block, 'sub', axis=1, tiled=True)  15.8 us
    gather x1, local copies, waits for them, and re-layouts, body(): copies_at = copies[:, obs_slot[0, 0]]  14.1 us
    all_to_all x1, starting transfers between devices, body(): lax.all_to_all(slot_ids, 'robot', split_axis=1, concat_axis=1, tiled=True)  7.28 us
    unnamed x32, local copies, waits for them, and re-layouts  7.06 us
    all_to_all x1, starting transfers between devices, body(): lax.all_to_all(outgoing, 'robot', split_axis=1, concat_axis=1, tiled=True)  6.01 us
    all_to_all x1, waiting for transfers between devices, body(): lax.all_to_all(outgoing, 'robot', split_axis=1, concat_axis=1, tiled=True)  5.69 us
  transfers between devices with their start and end apart: 3, of which 2 were waited for; matrix products, arithmetic and copies ran while one was open for 38% of the time, Pallas kernels for 0%

commit v1 on v0

--- a/solution.py
+++ b/solution.py
@@ -55,7 +55,7 @@
     residual_norms = jnp.sqrt(jnp.stack([primal_all, dual_all]) / landmark_total)
     pose_block = poses[0, 0]
     pose_count = pose_block.shape[1]
-    robot_all = lax.all_gather(pose_block, "sub", axis=1, tiled=True)
+    robot_all = jnp.concatenate(lax.all_gather(pose_block, "sub"), axis=1)
     pose_far = robot_all[:, edge_to[0, 0]]
     copies_at = copies[:, obs_slot[0, 0]]
     error = measurements[0, 0] - copies_at

time: 156 us -> 147 us (0.942)
  blocking collectives: 54.7 us -> 44.6 us
    all_gather x1, blocking collectives: 15.8 us -> 5.52 us  [body(): robot_all = jnp.concatenate(lax.all_gather(pose_block, 'sub'), axis=1)]
  transfers between devices with their start and end apart: 3 -> 3, of which waited for: 2 -> 2; matrix products, arithmetic and copies ran while one was open for 38% -> 41% of each run, Pallas kernels for 0% -> 0%
where the time goes in v1:
time: 147 us; the launch traced here: 146 us
  blocking collectives  44.6 us (30%)
  other arithmetic  40.4 us (27%)
  local copies, waits for them, and re-layouts  33 us (22%)
  starting transfers between devices  16.6 us (11%)
  waiting for transfers between devices  10.1 us (7%)
  between operations  1.65 us (1%)
    psum x1, blocking collectives, body(): primal_all, dual_all = lax.psum((primal, dualsum), ('robot', 'sub'))  39 us
    scatter-add x1, other arithmetic, body(): jax.ops.segment_sum(entries, pose_ids, num_segments=pose_count)  22.9 us
    gather x1, local copies, waits for them, and re-layouts, body(): copies_at = copies[:, obs_slot[0, 0]]  14.1 us
    unnamed x32, local copies, waits for them, and re-layouts  7.8 us
    all_to_all x1, starting transfers between devices, body(): lax.all_to_all(slot_ids, 'robot', split_axis=1, concat_axis=1, tiled=True)  7.28 us
    all_to_all x1, starting transfers between devices, body(): lax.all_to_all(outgoing, 'robot', split_axis=1, concat_axis=1, tiled=True)  6.01 us
    all_to_all x1, waiting for transfers between devices, body(): lax.all_to_all(outgoing, 'robot', split_axis=1, concat_axis=1, tiled=True)  5.69 us
    all_gather x1, blocking collectives, body(): robot_all = jnp.concatenate(lax.all_gather(pose_block, 'sub'), axis=1)  5.52 us
  transfers between devices with their start and end apart: 3, of which 2 were waited for; matrix products, arithmetic and copies ran while one was open for 41% of the time, Pallas kernels for 0%

profile of v1, /device:TPU:0, one launch (start us, length us, event | category | flops | bytes accessed | tf_op | source)
XLA Modules:
  0.0 146.3 jit_solution(16189412156546832474)
XLA Ops:
  1.1 1.3 reduce.16
  3.2 7.3 %all-to-all-start = ((s32[1,8,64]{2,0,1:T(1,128)}), s32[1,8,64]{2,0,1:T(1,128)S(1)}, u32[]{:S(2)}, u32[]{:S(2)}) async-start(s32[1,8,64]{2,0,1:T(1,128)} %all_to_all.22), calls=%async_computation | async-start | bytes 8192 | tf_op jit(solution)/shard_map/all_to_all | solution.py:39
  11.9 5.5 %all-gather = f32[4,1,6,1024]{3,1,2,0:T(1,128)S(1)} all-gather(f32[1,1,6,1024]{3,1,2,0:T(1,128)} %param.18), channel_id=2, replica_groups=mesh['robot'=8,'sub'=4] {'sub'}, dimensions={0}, use_global_device_ids=true | all-gather | bytes 122880 | tf_op jit(solution)/shard_map/all_gather | solution.py:58
  17.4 1.0 copy.59
  18.4 0.8 copy.56
  19.2 0.7 add_reduce_fusion.1
  20.8 1.4 copy.55
  22.2 14.1 %gather_fusion.1 = f32[4096,3]{1,0:T(8,128)} fusion(f32[3,512]{0,1:T(8,128)S(1)} %bitcast.59, s32[4096]{0:T(1024)S(1)} %broadcast_clamp_fusion), kind=kCustom, calls=%fused_computation.1 | custom fusion | bytes 114688 | tf_op jit(solution)/shard_map/gather | solution.py:60
  36.3 3.2 %bitcast_subtract_fusion = f32[3,4096]{0,1:T(8,128)} fusion(f32[4096,3]{1,0:T(8,128)} %gather_fusion.1, f32[1,1,3,4096]{2,3,1,0:T(8,128)S(1)} %copy.55), kind=kLoop, calls=%fused_computation.5 | loop fusion | flops 12288 | bytes 147456 | tf_op jit(solution)/shard_map/sub | solution.py:61
  39.5 2.3 %copy.57 = f32[3,4096]{1,0:T(4,128)S(1)} copy(f32[3,4096]{0,1:T(8,128)} %bitcast_subtract_fusion) | data formatting | bytes 98304 | tf_op jit(solution)/shard_map/sub | solution.py:61
  42.6 2.0 %copy.58 = f32[4096,6]{1,0:T(8,128)} copy(f32[4096,6]{0,1:T(8,128)S(1)} %bitcast.62) | data formatting | bytes 196608 | tf_op jit(solution)/shard_map/reduce_sum | solution.py:63
  45.3 1.0 copy.60
  46.4 2.8 %gather_fusion = f32[1024,6]{1,0:T(8,128)S(1)} fusion(f32[6,4096]{0,1:T(8,128)S(1)} %bitcast.60, s32[1024]{0:T(1024)S(1)} %broadcast_clamp_fusion.1), kind=kCustom, calls=%fused_computation | custom fusion | bytes 53248 | tf_op jit(solution)/shard_map/gather | solution.py:59
  49.2 22.9 %scatter_fusion = f32[6,1024]{0,1:T(8,128)S(1)} fusion(f32[6,1024]{0,1:T(8,128)S(1)} %bitcast.58, s32[4096]{0:T(1024)S(1)} %bitcast.73, f32[4096,6]{1,0:T(8,128)} %copy.58), kind=kCustom, calls=%fused_computation.3 | custom fusion | flops 24576 | bytes 311296 | tf_op jit(solution)/shard_map/vmap()/scatter-add | solution.py:66
  73.8 6.0 %all-to-all-start.1 = ((f32[8,1,256]{2,1,0:T(1,128)}), f32[8,1,256]{2,1,0:T(1,128)S(1)}, u32[]{:S(2)}, u32[]{:S(2)}) async-start(f32[8,1,256]{2,1,0:T(1,128)} %reshape.270), calls=%async_computation.1 | async-start | bytes 16384 | tf_op jit(solution)/shard_map/all_to_all | solution.py:38
  80.7 5.7 %all-to-all-done.1 = f32[8,1,256]{2,1,0:T(1,128)S(1)} async-done(((f32[8,1,256]{2,1,0:T(1,128)}), f32[8,1,256]{2,1,0:T(1,128)S(1)}, u32[]{:S(2)}, u32[]{:S(2)}) %all-to-all-start.1) | async-done | bytes 8224 | tf_op jit(solution)/shard_map/all_to_all | solution.py:38
  87.9 2.3 %scatter_custom_fusion.1 = f32[4,512]{0,1:T(8,128)S(1)} fusion(s32[512]{0:T(512)S(1)} %reshape.235, f32[512,4]{1,0:T(8,128)S(1)} %copy.65, f32[]{:T(128)} %constant.10.clone.1), kind=kCustom, calls=%fused_computation.21 | custom fusion | flops 2048 | bytes 8196 | tf_op jit(solution)/shard_map/vmap()/scatter-add | solution.py:42
  90.5 0.8 fusion
  91.3 1.0 gather_fusion.2
  93.2 3.3 %all-to-all-start.2 = ((f32[8,1,192]{2,1,0:T(1,128)}), f32[8,1,192]{2,1,0:T(1,128)S(1)}, u32[]{:S(2)}, u32[]{:S(2)}) async-start(f32[8,1,192]{2,1,0:T(1,128)} %reshape.272), calls=%async_computation.2 | async-start | bytes 16384 | tf_op jit(solution)/shard_map/all_to_all | solution.py:47
  98.6 4.4 %all-to-all-done.2 = f32[8,1,192]{2,1,0:T(1,128)S(1)} async-done(((f32[8,1,192]{2,1,0:T(1,128)}), f32[8,1,192]{2,1,0:T(1,128)S(1)}, u32[]{:S(2)}, u32[]{:S(2)}) %all-to-all-start.2) | async-done | bytes 6176 | tf_op jit(solution)/shard_map/all_to_all | solution.py:47
  104.0 0.7 fusion.4
  105.3 39.0 %all-reduce = (f32[1]{0:T(128)}, f32[1]{0:T(128)}) all-reduce(f32[1]{0:T(128)} %bitcast.24, f32[1]{0:T(128)} %bitcast.23), channel_id=1, replica_groups=mesh['robot'=8,'sub'=4] {'robot','sub'}, use_global_device_ids=true, to_apply=%region_7.0 | all-reduce | flops 2 | bytes 16 | tf_op jit(solution)/shard_map/psum | solution.py:53
  144.4 1.9 %fusion.10 = f32[2]{0:T(128)} fusion(f32[1]{0:T(128)} %get-tuple-element.22, f32[1]{0:T(128)} %get-tuple-element.23), kind=kLoop, calls=%fused_computation.42 | loop fusion | flops 4 | bytes 16 | tf_op jit(solution)/shard_map/sqrt | solution.py:55
  (69 shorter events, 13.0 us)
Async XLA Ops:
  3.2 70.6 %all-to-all-start = ((s32[1,8,64]{2,0,1:T(1,128)}), s32[1,8,64]{2,0,1:T(1,128)S(1)}, u32[]{:S(2)}, u32[]{:S(2)}) async-start(s32[1,8,64]{2,0,1:T(1,128)} %all_to_all.22), calls=%async_computation | async-start | bytes 8192 | tf_op jit(solution)/shard_map/all_to_all | solution.py:39
  39.5 2.3 %copy-start.1 = (f32[1,1,18,4096]{3,1,2,0:T(1,128)S(1)}, f32[1,1,18,4096]{3,1,2,0:T(1,128)}, u32[]{:S(2)}) copy-start(f32[1,1,18,4096]{3,1,2,0:T(1,128)} %param.20) | copy-start | bytes 884740
  42.6 2.7 %copy-start.9 = (s32[1,1,1024]{2,1,0:T(1,128)S(1)}, s32[1,1,1024]{2,1,0:T(1,128)}, u32[]{:S(2)}) copy-start(s32[1,1,1024]{2,1,0:T(1,128)} %param.24) | copy-start | bytes 12292
  42.6 2.7 %copy-start.5 = (f32[1,1,6,1024]{3,1,2,0:T(1,128)S(1)}, f32[1,1,6,1024]{3,1,2,0:T(1,128)}, u32[]{:S(2)}) copy-start(f32[1,1,6,1024]{3,1,2,0:T(1,128)} %param.25) | copy-start | bytes 73732
  44.6 4.6 %copy-start.7 = (s32[1,1,4096]{2,1,0:T(1,128)S(1)}, s32[1,1,4096]{2,1,0:T(1,128)}, u32[]{:S(2)}) copy-start(s32[1,1,4096]{2,1,0:T(1,128)} %param.22) | copy-start | bytes 49156
  49.2 23.0 %copy-start = (f32[1,1,6,1024]{2,3,1,0:T(8,128)S(1)}, f32[1,1,6,1024]{2,3,1,0:T(8,128)}, u32[]{:S(2)}) copy-start(f32[1,1,6,1024]{2,3,1,0:T(8,128)} %copy.60) | copy-start | bytes 73732
  49.2 23.2 %copy-start.3 = (f32[1,1,36,1024]{3,1,2,0:T(1,128)S(1)}, f32[1,1,36,1024]{3,1,2,0:T(1,128)}, u32[]{:S(2)}) copy-start(f32[1,1,36,1024]{3,1,2,0:T(1,128)} %param.19) | copy-start | bytes 442372
  72.1 1.5 %copy-start.8 = (f32[1,1,3,512]{3,1,2,0:T(1,128)S(1)}, f32[1,1,3,512]{3,1,2,0:T(1,128)}, u32[]{:S(2)}) copy-start(f32[1,1,3,512]{3,1,2,0:T(1,128)} %param.17) | copy-start | bytes 18436
  72.2 24.3 %copy-start.2 = (f32[1,1,6,1024]{3,1,2,0:T(1,128)S(1)}, f32[1,1,6,1024]{3,1,2,0:T(1,128)}, u32[]{:S(2)}) copy-start(f32[1,1,6,1024]{3,1,2,0:T(1,128)} %param.18) | copy-start | bytes 73732
  72.8 31.9 %copy-start.4 = (f32[1,1,3,512]{3,1,2,0:T(1,128)S(1)}, f32[1,1,3,512]{3,1,2,0:T(1,128)}, u32[]{:S(2)}) copy-start(f32[1,1,3,512]{3,1,2,0:T(1,128)} %param.13) | copy-start | bytes 18436
  72.8 31.9 %copy-start.6 = (f32[1,1,3,512]{3,1,2,0:T(1,128)S(1)}, f32[1,1,3,512]{3,1,2,0:T(1,128)}, u32[]{:S(2)}) copy-start(f32[1,1,3,512]{3,1,2,0:T(1,128)} %param.14) | copy-start | bytes 18436
  73.8 12.5 %all-to-all-start.1 = ((f32[8,1,256]{2,1,0:T(1,128)}), f32[8,1,256]{2,1,0:T(1,128)S(1)}, u32[]{:S(2)}, u32[]{:S(2)}) async-start(f32[8,1,256]{2,1,0:T(1,128)} %reshape.270), calls=%async_computation.1 | async-start | bytes 16384 | tf_op jit(solution)/shard_map/all_to_all | solution.py:38
  93.2 9.8 %all-to-all-start.2 = ((f32[8,1,192]{2,1,0:T(1,128)}), f32[8,1,192]{2,1,0:T(1,128)S(1)}, u32[]{:S(2)}, u32[]{:S(2)}) async-start(f32[8,1,192]{2,1,0:T(1,128)} %reshape.272), calls=%async_computation.2 | async-start | bytes 16384 | tf_op jit(solution)/shard_map/all_to_all | solution.py:47
